TPU v7x, 32 devices: a whole 2x2x4 slice. The times are simulated.
32 devices in a mesh: row: 8 (over z, y), col: 4 (over x, core).
Axes of the slice: x: 2, y: 2, z: 4, core: 2. Of those that a mesh axis runs over, the one named last changes fastest.
Arguments:
- expression: bfloat16 [4096, 1024], P(('row', 'col')), as said below
- power_order: int32 [20], replicated, may hold values from 0 to 19, each once
Outputs:
- log_conn: float32 [4096, 20], P(('row', 'col'))
- fit: float32 [20], replicated
- slope: float32 [20], replicated
Inputs may be any that keep to these rules, and one draw needn't show every extreme that they name: `expression`: each gene's row has mean zero and unit variance over the samples, up to rounding.
All inputs are finite; a program needn't handle non-finite values.
Results may differ from a plain program's by a relative error of at most 0.0029.
Values may be sent and summed in bfloat16 or wider, within the bound.
No kernel may reach another device: no remote copies, remote signals or barrier semaphores. Data moves between devices by JAX's collectives and lax.ppermute only.
A program may use at most 64 MiB of HBM per device.

v0:
```python
import math
import jax
import jax.numpy as jnp
from jax import lax
from jax.sharding import PartitionSpec as P


def power_sums(rows, partners, samples, powers):
    corr = (
        lax.dot_general(
            rows, partners, (((1,), (1,)), ((), ())), preferred_element_type=jnp.float32
        )
        / samples
    )
    magnitude = jnp.abs(corr)
    current = magnitude
    sums = []
    for power in range(powers):
        sums.append(jnp.sum(current, axis=1))
        current = current * magnitude
    return jnp.stack(sums, axis=1)


def scale_free_fit(hist, log_total, bins):
    centers = jnp.arange(bins, dtype=jnp.float32) * (log_total / (bins - 1))
    weight_sum = jnp.sum(hist, axis=1, keepdims=True)
    ylog = jnp.log(hist + 1.0) - log_total
    xmean = jnp.sum(hist * centers[None, :], axis=1, keepdims=True) / weight_sum
    ymean = jnp.sum(hist * ylog, axis=1, keepdims=True) / weight_sum
    xdev = centers[None, :] - xmean
    ydev = ylog - ymean
    sxx = jnp.maximum(jnp.sum(hist * xdev * xdev, axis=1) / weight_sum[:, 0], 0.05)
    syy = jnp.maximum(jnp.sum(hist * ydev * ydev, axis=1) / weight_sum[:, 0], 0.05)
    sxy = jnp.sum(hist * xdev * ydev, axis=1) / weight_sum[:, 0]
    return (-sxy * jnp.abs(sxy) / (sxx * syy), sxy / sxx)


def on_device(expression, power_order):
    samples = expression.shape[1]
    powers = power_order.shape[0]
    bins = 128
    genes_total = expression.shape[0] * lax.axis_size("row") * lax.axis_size("col")
    panel = lax.all_gather(expression, "col", axis=0, tiled=True)
    partial_value = power_sums(
        panel, lax.all_gather(expression, "row", axis=0, tiled=True), samples, powers
    )
    conn = lax.psum_scatter(partial_value, "col", scatter_dimension=0, tiled=True)
    selector = (power_order[:, None] == jnp.arange(powers, dtype=jnp.int32)[None, :]).astype(
        jnp.float32
    )
    picked = jnp.dot(conn, selector.T, precision=lax.Precision.HIGHEST)
    log_conn = jnp.log(picked)
    log_total = math.log(genes_total)
    position = log_conn * ((bins - 1) / log_total)
    levels = jnp.arange(bins, dtype=jnp.float32)
    weights = jnp.maximum(0.0, 1.0 - jnp.abs(position[:, :, None] - levels[None, None, :]))
    local_hist = jnp.sum(weights, axis=0)
    hist = lax.psum(local_hist, ("row", "col"))
    fit, slope = scale_free_fit(hist, log_total, bins)
    return (log_conn, fit, slope)


def solution(mesh):
    placed = (P(("row", "col"), None), P())
    return jax.shard_map(
        on_device,
        mesh=mesh,
        in_specs=placed,
        out_specs=(P(("row", "col"), None), P(), P()),
        check_vma=False,
    )
```

profile of v0, /device:TPU:0, one launch (start us, length us, event | category | flops | bytes accessed | tf_op | source)
XLA Modules:
  0.0 156.3 jit_solution(5682563446341147419)
XLA Ops:
  7.2 0.0 all-gather.3.cloned.1.call-start
  7.2 0.7 all-gather.3.cloned.1.call-update
  7.9 0.0 all-gather.5.cloned.1.call-start
  7.9 0.7 all-gather.5.cloned.1.call-update
  8.6 0.0 copy-start
  8.7 0.0 reduce-scatter.2.cloned.1.call-start
  8.7 20.3 %all-gather.3.cloned.1.call-done = bf16[512,1024]{1,0:T(8,128)(2,1)} async-done(((bf16[128,1024]{1,0:T(8,128)(2,1)}), bf16[512,1024]{1,0:T(8,128)(2,1)}) %all-gather.3.cloned.1.call-update) | async-done | bytes 1048592 | tf_op jit(solution)/shard_map/all_gather | solution.py:43
  29.0 51.3 %all-gather.5.cloned.1.call-done = bf16[1024,1024]{1,0:T(8,128)(2,1)} async-done(((bf16[128,1024]{1,0:T(8,128)(2,1)}), bf16[1024,1024]{1,0:T(8,128)(2,1)}) %all-gather.5.cloned.1.call-update) | async-done | bytes 2097168 | tf_op jit(solution)/shard_map/all_gather | solution.py:45
  80.2 6.5 %multiply_reduce_fusion = (f32[512]{0:T(512)S(1)}, f32[512]{0:T(512)S(1)}, f32[512]{0:T(512)S(1)}, f32[512]{0:T(512)S(1)}, f32[512]{0:T(512)S(1)}, /*index=5*/f3...) fusion(bf16[512,1024]{1,0:T(8,128)(2,1)} %all-gather.3.cloned.1, ...), kind=kOutput, calls=%fused_computation | convolution fusion | flops 1095227392 | bytes 3186688 | tf_op jit(solution)/shard_map/dot_general | solution.py:10
  86.8 1.9 %stack.83 = f32[512,20]{0,1:T(8,128)} concatenate(f32[512,1]{0,1:T(1,128)S(1)} %bitcast.42, f32[512,1]{0,1:T(1,128)S(1)} %bitcast.41, f32[512,1]{0,1:T(1,128)S(1)} %bitcast.39, f32[512,1]{0,1:T(1,128)S(1)} %bitcast.40, f32[512,1]{0,1:T(1,128)S(1)} %bitcast.35, f32[512,1]{0,1:T(1,128)S(1)} %bitcast.36, f32[512,1]{0,1:T(1,128)S(1)} %bitcast.38, f32[512,1]{0,1:T(1,128)S(1)} %bitcast.37, ...), dimensions={1} | concatenate | bytes 81920 | tf_op jit(solution)/shard_map/stack | solution.py:21
  88.7 0.0 reduce-scatter.2.cloned.1.call-update
  88.7 18.2 %reduce-scatter.2.cloned.1.call-done = f32[128,20]{0,1:T(8,128)} async-done(((f32[512,20]{0,1:T(8,128)}), f32[128,20]{0,1:T(8,128)}) %reduce-scatter.2.cloned.1.call-update) | async-done | bytes 10256 | tf_op jit(solution)/shard_map/reduce_scatter | solution.py:47
  106.9 0.0 copy-done
  106.9 1.5 broadcast_multiply_fusion
  108.4 0.4 maximum_reduce_fusion
  108.8 39.5 %psum.7 = f32[20,128]{1,0:T(8,128)S(1)} all-reduce(f32[20,128]{1,0:T(8,128)S(1)} %maximum_reduce_fusion), channel_id=1, replica_groups=mesh['row'=8,'col'=4] {'row','col'}, use_global_device_ids=true, to_apply=%region_22.0 | all-reduce | flops 2560 | bytes 20480 | tf_op jit(solution)/shard_map/psum | solution.py:58
  148.3 0.2 multiply_reduce_fusion.11
  148.5 0.2 multiply_reduce_fusion.10
  148.7 0.5 multiply_divide_fusion
  149.2 0.5 multiply_divide_fusion.1
  (2 shorter events, 0.0 us)
Async XLA Ops:
  7.2 21.8 %all-gather.3.cloned.1.call-start = ((), (), s32[]{:S(2)}) async-start(), calls=%async_computation.1 | async-start | bytes 1310720 | tf_op jit(solution)/shard_map/all_gather | solution.py:43
  7.9 72.3 %all-gather.5.cloned.1.call-start = ((), (), s32[]{:S(2)}) async-start(), calls=%async_computation.2 | async-start | bytes 2359296 | tf_op jit(solution)/shard_map/all_gather | solution.py:45
  8.6 98.3 %copy-start = (s32[20]{0:T(128)S(1)}, s32[20]{0:T(128)}, u32[]{:S(2)}) copy-start(s32[20]{0:T(128)} %param.3) | copy-start | bytes 244
  8.7 98.2 %reduce-scatter.2.cloned.1.call-start = ((), (), s32[]{:S(2)}) async-start(), calls=%async_computation.3 | async-start | bytes 61440 | tf_op jit(solution)/shard_map/reduce_scatter | solution.py:47
Sparse Core Ops, SparseCore 0:
  9.5 19.4 all-gather.2
  31.1 49.0 all-gather.4
  88.8 18.0 reduce-scatter.1
where the time goes:
time: 157 us; the launch traced here: 156 us
  waiting for transfers between devices  91.1 us (58%)
  blocking collectives  39.5 us (25%)
  between operations  13.8 us (9%)
  matrix products  8.05 us (5%)
  local copies, waits for them, and re-layouts  1.88 us (1%)
  other arithmetic  1.88 us (1%)
    all_gather x1, waiting for transfers between devices, on_device(): lax.all_gather(expression, 'row', axis=0, tiled=True)  51.3 us
    psum x1, blocking collectives, on_device(): hist = lax.psum(local_hist, ('row', 'col'))  39.5 us
    all_gather x1, waiting for transfers between devices, on_device(): panel = lax.all_gather(expression, 'col', axis=0, tiled=True)  20.3 us
    reduce_scatter x1, waiting for transfers between devices, on_device(): lax.psum_scatter(partial_value, 'col', scatter_dimension=0, tiled=True)  18.2 us
    dot_general x1, matrix products, power_sums(): lax.dot_general(rows, partners, (((1,), (1,)), ((), ())), preferred_eleme...  6.54 us
  transfers between devices with their start and end apart: 3, of which 3 were waited for; matrix products, arithmetic and copies ran while one was open for 0% of the time, Pallas kernels for 0%

commit v1 on v0

--- a/solution.py
+++ b/solution.py
@@ -55,7 +55,7 @@
     levels = jnp.arange(bins, dtype=jnp.float32)
     weights = jnp.maximum(0.0, 1.0 - jnp.abs(position[:, :, None] - levels[None, None, :]))
     local_hist = jnp.sum(weights, axis=0)
-    hist = lax.psum(local_hist, ("row", "col"))
+    hist = lax.psum(lax.psum(local_hist, axis_name="col"), axis_name="row")
     fit, slope = scale_free_fit(hist, log_total, bins)
     return (log_conn, fit, slope)
 

time: 157 us -> 164 us (1.045)
  blocking collectives: 39.5 us -> 47.3 us
    psum x1 -> x2, blocking collectives: 39.5 us -> 47.3 us  [on_device(): hist = lax.psum(lax.psum(local_hist, axis_name='col'), axis_name='row')]
where the time goes in v1:
time: 164 us
  waiting for transfers between devices  91.1 us (56%)
  blocking collectives  47.3 us (29%)
  between operations  13.8 us (8%)
  matrix products  8.05 us (5%)
  local copies, waits for them, and re-layouts  1.88 us (1%)
  other arithmetic  1.88 us (1%)
    all_gather x1, waiting for transfers between devices, on_device(): lax.all_gather(expression, 'row', axis=0, tiled=True)  51.3 us
    psum x2, blocking collectives, on_device(): hist = lax.psum(lax.psum(local_hist, axis_name='col'), axis_name='row')  47.3 us
    all_gather x1, waiting for transfers between devices, on_device(): panel = lax.all_gather(expression, 'col', axis=0, tiled=True)  20.3 us
    reduce_scatter x1, waiting for transfers between devices, on_device(): lax.psum_scatter(partial_value, 'col', scatter_dimension=0, tiled=True)  18.2 us
    dot_general x1, matrix products, power_sums(): lax.dot_general(rows, partners, (((1,), (1,)), ((), ())), preferred_eleme...  6.54 us
  transfers between devices with their start and end apart: 3, of which 3 were waited for; matrix products, arithmetic and copies ran while one was open for 0% of the time, Pallas kernels for 0%

profile of v1, /device:TPU:0, one launch (start us, length us, event | category | flops | bytes accessed | tf_op | source)
XLA Modules:
  0.0 164.1 jit_solution(18399924165479159366)
XLA Ops:
  7.2 0.0 all-gather.3.cloned.1.call-start
  7.2 0.7 all-gather.3.cloned.1.call-update
  7.9 0.0 all-gather.5.cloned.1.call-start
  7.9 0.7 all-gather.5.cloned.1.call-update
  8.6 0.0 copy-start
  8.7 0.0 reduce-scatter.2.cloned.1.call-start
  8.7 20.3 %all-gather.3.cloned.1.call-done = bf16[512,1024]{1,0:T(8,128)(2,1)} async-done(((bf16[128,1024]{1,0:T(8,128)(2,1)}), bf16[512,1024]{1,0:T(8,128)(2,1)}) %all-gather.3.cloned.1.call-update) | async-done | bytes 1048592 | tf_op jit(solution)/shard_map/all_gather | solution.py:43
  29.0 51.3 %all-gather.5.cloned.1.call-done = bf16[1024,1024]{1,0:T(8,128)(2,1)} async-done(((bf16[128,1024]{1,0:T(8,128)(2,1)}), bf16[1024,1024]{1,0:T(8,128)(2,1)}) %all-gather.5.cloned.1.call-update) | async-done | bytes 2097168 | tf_op jit(solution)/shard_map/all_gather | solution.py:45
  80.2 6.5 %multiply_reduce_fusion = (f32[512]{0:T(512)S(1)}, f32[512]{0:T(512)S(1)}, f32[512]{0:T(512)S(1)}, f32[512]{0:T(512)S(1)}, f32[512]{0:T(512)S(1)}, /*index=5*/f3...) fusion(bf16[512,1024]{1,0:T(8,128)(2,1)} %all-gather.3.cloned.1, ...), kind=kOutput, calls=%fused_computation | convolution fusion | flops 1095227392 | bytes 3186688 | tf_op jit(solution)/shard_map/dot_general | solution.py:10
  86.8 1.9 %stack.83 = f32[512,20]{0,1:T(8,128)} concatenate(f32[512,1]{0,1:T(1,128)S(1)} %bitcast.42, f32[512,1]{0,1:T(1,128)S(1)} %bitcast.41, f32[512,1]{0,1:T(1,128)S(1)} %bitcast.39, f32[512,1]{0,1:T(1,128)S(1)} %bitcast.40, f32[512,1]{0,1:T(1,128)S(1)} %bitcast.35, f32[512,1]{0,1:T(1,128)S(1)} %bitcast.36, f32[512,1]{0,1:T(1,128)S(1)} %bitcast.38, f32[512,1]{0,1:T(1,128)S(1)} %bitcast.37, ...), dimensions={1} | concatenate | bytes 81920 | tf_op jit(solution)/shard_map/stack | solution.py:21
  88.7 0.0 reduce-scatter.2.cloned.1.call-update
  88.7 18.2 %reduce-scatter.2.cloned.1.call-done = f32[128,20]{0,1:T(8,128)} async-done(((f32[512,20]{0,1:T(8,128)}), f32[128,20]{0,1:T(8,128)}) %reduce-scatter.2.cloned.1.call-update) | async-done | bytes 10256 | tf_op jit(solution)/shard_map/reduce_scatter | solution.py:47
  106.9 0.0 copy-done
  106.9 1.5 broadcast_multiply_fusion
  108.4 0.4 maximum_reduce_fusion
  108.8 10.1 %psum.14 = f32[20,128]{1,0:T(8,128)S(1)} all-reduce(f32[20,128]{1,0:T(8,128)S(1)} %maximum_reduce_fusion), channel_id=1, replica_groups=mesh['row'=8,'col'=4] {'col'}, use_global_device_ids=true, to_apply=%region_22.0 | all-reduce | flops 2560 | bytes 20480 | tf_op jit(solution)/shard_map/psum | solution.py:58
  119.0 37.1 %psum.15 = f32[20,128]{1,0:T(8,128)S(1)} all-reduce(f32[20,128]{1,0:T(8,128)S(1)} %psum.14), channel_id=1, replica_groups=mesh['row'=8,'col'=4] {'row'}, use_global_device_ids=true, to_apply=%region_23.0 | all-reduce | flops 2560 | bytes 20480 | tf_op jit(solution)/shard_map/psum | solution.py:58
  156.1 0.2 multiply_reduce_fusion.11
  156.3 0.2 multiply_reduce_fusion.10
  156.5 0.5 multiply_divide_fusion
  157.0 0.5 multiply_divide_fusion.1
  (2 shorter events, 0.0 us)
Async XLA Ops:
  7.2 21.8 %all-gather.3.cloned.1.call-start = ((), (), s32[]{:S(2)}) async-start(), calls=%async_computation.1 | async-start | bytes 1310720 | tf_op jit(solution)/shard_map/all_gather | solution.py:43
  7.9 72.3 %all-gather.5.cloned.1.call-start = ((), (), s32[]{:S(2)}) async-start(), calls=%async_computation.2 | async-start | bytes 2359296 | tf_op jit(solution)/shard_map/all_gather | solution.py:45
  8.6 98.3 %copy-start = (s32[20]{0:T(128)S(1)}, s32[20]{0:T(128)}, u32[]{:S(2)}) copy-start(s32[20]{0:T(128)} %param.3) | copy-start | bytes 244
  8.7 98.2 %reduce-scatter.2.cloned.1.call-start = ((), (), s32[]{:S(2)}) async-start(), calls=%async_computation.3 | async-start | bytes 61440 | tf_op jit(solution)/shard_map/reduce_scatter | solution.py:47
Sparse Core Ops, SparseCore 0:
  9.5 19.4 all-gather.2
  31.1 49.0 all-gather.4
  88.8 18.0 reduce-scatter.1
